TPU v7x, 512 devices: a whole 4x8x8 slice. The times are simulated.
512 devices in a mesh: rep: 32 (over x, z), tp: 16 (over y, core).
Axes of the slice: x: 4, y: 8, z: 8, core: 2. Of those that a mesh axis runs over, the one named last changes fastest.
Arguments:
- prompt_queries: bfloat16 [15872, 4096], P('rep', 'tp'), parts along dimension 0, may hold values from -240 to 240
- prompt_entries: bfloat16 [64, 496, 512], P('rep', 'tp'), parts along dimension 0, may hold values from -6 to 6
- history_cache: bfloat16 [64, 1024, 512], P('rep', 'tp'), parts along dimension 0, may hold values from -6 to 6
- decode_queries: bfloat16 [512, 4096], P('rep', 'tp'), parts along dimension 0, may hold values from -240 to 240
- decode_entries: bfloat16 [64, 16, 512], P('rep'), parts along dimension 0, may hold values from -6 to 6
- decode_cache: bfloat16 [64, 16, 768, 512], P('rep', None, 'tp'), parts along dimension 0, may hold values from -6 to 6
- decode_lengths: int32 [512], P('rep'), parts along dimension 0, may hold values from 1 to 768
- prompt_start: int32 [32], P('rep'), parts along dimension 0, may hold values from 512 to 1024
- out_weight: bfloat16 [4096, 4096], P('tp'), may hold values from -0.09375 to 0.09375
- residual: bfloat16 [512, 131072], P('tp', 'rep'), parts along dimension 1, may hold values from -4 to 4
- norm_gain: float32 [4096], replicated, may hold values from 0.5 to 1.5
Outputs:
- new_residual: bfloat16 [512, 131072], P('tp', 'rep'), parts along dimension 1
- normed: bfloat16 [512, 131072], P('tp', 'rep'), parts along dimension 1
There are 32 independent parts, one for each index of `rep`. A program takes and returns all parts, laid end to end along the dimension named above; an argument that names none is the same for every part. Nothing has to cross between parts.
Inputs may be any that keep to these rules, and one draw needn't show every extreme that they name: The rows of history_cache at and past prompt_start are not read. `decode_lengths`: rows of decode_cache at and past a request's length are not read.
All inputs are finite; a program needn't handle non-finite values.
Results may differ from a plain program's by a relative error of at most 0.017.
Values may be sent and summed in bfloat16 or wider, within the bound.
A program may use at most 64 MiB of HBM per device.

v0:
```python
import jax
import jax.numpy as jnp
from jax import lax
from jax.sharding import PartitionSpec as P

HEADS = 32
KV_HEADS = 4
HEAD_DIM = 128


lowest_score = -1e30


def copy_for_each(shard, axis):
    copies = jnp.broadcast_to(shard, (lax.axis_size(axis), *shard.shape))
    return lax.all_to_all(copies, axis, split_axis=0, concat_axis=0, tiled=True)


def joined_along(tiles, dim):
    dims = list(tiles.shape[1:])
    dims[dim] *= tiles.shape[0]
    return jnp.moveaxis(tiles, 0, dim).reshape(dims)


def gather_directly(shard, axis, dim):
    tiles = copy_for_each(shard, axis)
    return joined_along(tiles, dim)


def in_one_piece(arrays, axis, split_dim, concat_dim, along):
    columns = [a.reshape(*a.shape[:along], -1) for a in arrays]
    both = jnp.concatenate(columns, axis=along)
    filled, at, outs = (
        lax.all_to_all(both, axis, split_axis=split_dim, concat_axis=concat_dim, tiled=True),
        0,
        [],
    )
    for a, column in zip(arrays, columns):
        slab = filled[..., at : at + column.shape[along]]
        outs.append(slab.reshape(*slab.shape[:along], *a.shape[along:]))
        at += column.shape[along]
    return tuple(outs)


def absorb(carry, queries, keys, values, valid, scale):
    highest, totals, summed = carry
    scores = jnp.einsum("thd,phd->thp", queries, keys, preferred_element_type=jnp.float32) * scale
    masked = jnp.where(valid[:, None, :], scores, lowest_score)
    raised = jnp.maximum(highest, jnp.max(masked, axis=-1))
    weights = jnp.where(valid[:, None, :], jnp.exp(scores - raised[..., None]), 0.0)
    factor = jnp.exp(highest - raised)
    totals = totals * factor + jnp.sum(weights, axis=-1)
    summed = summed * factor[..., None] + jnp.einsum(
        "thp,phd->thd", weights.astype(jnp.bfloat16), values, preferred_element_type=jnp.float32
    )
    return (raised, totals, summed)


def per_device(
    prompt_queries,
    prompt_entries,
    history_cache,
    decode_queries,
    decode_entries,
    decode_cache,
    decode_lengths,
    prompt_start,
    out_weight,
    residual,
    norm_gain,
):
    scale = HEAD_DIM ** (-0.5)
    group = HEADS // KV_HEADS
    local_heads = prompt_queries.shape[1] // HEAD_DIM
    first_head = lax.axis_index("tp") * local_heads
    key_index = (first_head + jnp.arange(local_heads, dtype=jnp.int32)) // group
    prompt_rows = prompt_queries.shape[0]
    queries = prompt_queries.reshape(prompt_rows, local_heads, HEAD_DIM)
    offset = prompt_start[0]
    row_places = jnp.arange(prompt_rows, dtype=jnp.int32)
    begin = (
        jnp.full((prompt_rows, local_heads), lowest_score, jnp.float32),
        jnp.zeros((prompt_rows, local_heads), jnp.float32),
        jnp.zeros((prompt_rows, local_heads, HEAD_DIM), jnp.float32),
    )
    devices = lax.axis_size("tp")
    owned_heads = max(1, local_heads // group)
    targets = (
        jnp.arange(devices, dtype=jnp.int32)[:, None] * local_heads // group
        + jnp.arange(owned_heads, dtype=jnp.int32)[None, :]
    )

    def spread(block):
        rows_here = block.shape[1]
        shaped = block.reshape(2, rows_here, KV_HEADS, HEAD_DIM)
        return jnp.take(shaped, targets.reshape(-1), axis=2).reshape(
            2, rows_here, devices, owned_heads, HEAD_DIM
        )

    history_own, prompt_own = (
        lax.all_to_all(spread(history_cache), "tp", split_axis=2, concat_axis=1, tiled=True),
        lax.all_to_all(spread(prompt_entries), "tp", split_axis=2, concat_axis=1, tiled=True),
    )
    local_slot = key_index - first_head // group

    def own_heads(block):
        shaped = block.reshape(2, block.shape[1], owned_heads, HEAD_DIM)
        return jnp.take(shaped, local_slot, axis=2)

    history_kv = own_heads(history_own)
    prompt_kv = own_heads(prompt_own)
    history_places = jnp.arange(history_kv.shape[1], dtype=jnp.int32)
    carry = absorb(
        begin, queries, history_kv[0], history_kv[1], (history_places < offset)[None, :], scale
    )
    prompt_places = jnp.arange(prompt_kv.shape[1], dtype=jnp.int32)
    prompt_valid = prompt_places[None, :] <= row_places[:, None]
    highest, totals, summed = absorb(
        carry, queries, prompt_kv[0], prompt_kv[1], prompt_valid, scale
    )
    prompt_out = (
        (summed / totals[..., None])
        .astype(jnp.bfloat16)
        .reshape(prompt_rows, local_heads * HEAD_DIM)
    )
    decode_rows = decode_queries.shape[0]
    span = decode_cache.shape[2]
    every_query = gather_directly(decode_queries, "tp", 1)
    grouped = every_query.reshape(decode_rows, KV_HEADS, group, HEAD_DIM)
    cache_keys = decode_cache[0].reshape(decode_rows, span, KV_HEADS, HEAD_DIM)
    cache_values = decode_cache[1].reshape(decode_rows, span, KV_HEADS, HEAD_DIM)
    places = lax.axis_index("tp") * span + jnp.arange(span, dtype=jnp.int32)
    valid = (places[None, :] < decode_lengths[:, None])[:, None, None, :]
    scores = (
        jnp.einsum("bkgd,bpkd->bkgp", grouped, cache_keys, preferred_element_type=jnp.float32)
        * scale
    )
    local_top = jnp.max(jnp.where(valid, scores, lowest_score), axis=-1)
    weights = jnp.where(valid, jnp.exp(scores - local_top[..., None]), 0.0)
    local_totals = jnp.sum(weights, axis=-1)
    local_summed = jnp.einsum(
        "bkgp,bpkd->bkgd",
        weights.astype(jnp.bfloat16),
        cache_values,
        preferred_element_type=jnp.float32,
    )
    local_top = local_top.reshape(decode_rows, HEADS)
    local_totals = local_totals.reshape(decode_rows, HEADS)
    local_summed = local_summed.reshape(decode_rows, HEADS, HEAD_DIM)
    parts_top, parts_totals, parts_summed = in_one_piece(
        (local_top[None], local_totals[None], local_summed[None]), "tp", 2, 0, 3
    )
    top_heads = jnp.max(parts_top, axis=0)
    factor = jnp.exp(parts_top - top_heads[None])
    totals_heads = jnp.sum(parts_totals * factor, axis=0)
    summed_heads = jnp.sum(parts_summed * factor[..., None], axis=0)
    own_query = decode_queries.reshape(decode_rows, local_heads, HEAD_DIM)
    shaped = decode_entries.reshape(decode_entries.shape[:-1] + (KV_HEADS, HEAD_DIM))
    fresh = jnp.take(shaped, key_index, axis=-2)
    own_score = (
        jnp.sum(own_query.astype(jnp.float32) * fresh[0].astype(jnp.float32), axis=-1) * scale
    )
    combined_top = jnp.maximum(top_heads, own_score)
    factor = jnp.exp(top_heads - combined_top)
    own_weight = jnp.exp(own_score - combined_top)
    own_rounded = lax.optimization_barrier(own_weight.astype(jnp.bfloat16)).astype(jnp.float32)
    totals_heads = totals_heads * factor + own_weight
    summed_heads = summed_heads * factor[..., None] + own_rounded[..., None] * fresh[1].astype(
        jnp.float32
    )
    decode_out = (
        (summed_heads / totals_heads[..., None])
        .astype(jnp.bfloat16)
        .reshape(decode_rows, local_heads * HEAD_DIM)
    )
    attended = jnp.concatenate([prompt_out, decode_out], axis=0)
    projected = lax.psum_scatter(
        jnp.dot(attended, out_weight, preferred_element_type=jnp.float32).astype(jnp.bfloat16),
        "tp",
        scatter_dimension=0,
        tiled=True,
    ).astype(jnp.float32)
    hidden = residual.astype(jnp.float32) + projected
    mean_square = jnp.mean(hidden * hidden, axis=-1, keepdims=True)
    normed = (hidden * lax.rsqrt(mean_square + 1e-05) * norm_gain).astype(jnp.bfloat16)
    return (hidden.astype(jnp.bfloat16), normed)


def solution(mesh):
    placed = (
        P("rep", "tp"),
        P("rep", "tp", None),
        P("rep", "tp", None),
        P("rep", "tp"),
        P("rep", None, None),
        P("rep", None, "tp", None),
        P("rep"),
        P("rep"),
        P("tp", None),
        P("tp", "rep"),
        P(),
    )
    return jax.shard_map(
        per_device,
        mesh=mesh,
        in_specs=placed,
        out_specs=(P("tp", "rep"), P("tp", "rep")),
        check_vma=False,
    )
```

profile of v0, /device:TPU:1, one launch (start us, length us, event | category | flops | bytes accessed | tf_op | source)
XLA Modules:
  0.0 180.2 jit_solution(16465273084862838202)
XLA Ops:
  7.2 1.5 broadcast_in_dim.154
  8.7 10.1 %all-to-all-start.2 = ((bf16[16,16,256]{2,1,0:T(8,128)(2,1)}), bf16[16,16,256]{2,1,0:T(8,128)(2,1)S(1)}, u32[]{:S(2)}, u32[]{:S(2)}) async-start(bf16[16,16,256]{2,1,0:T(8,128)(2,1)} %broadcast_in_dim.154), calls=%async_computation.2 | async-start | bytes 262144 | tf_op jit(solution)/shard_map/all_to_all | solution.py:16
  21.6 1.4 fusion.53
  26.4 1.9 %gather_fusion.1 = bf16[16,2,31,128]{3,1,2,0:T(2,128)(2,1)} fusion(bf16[2,31,4,128]{3,0,2,1:T(2,128)(2,1)S(1)} %bitcast.195, s32[1024]{0:T(1024)S(1)} %pad_clamp_fusion.1), kind=kCustom, calls=%fused_computation.1 | custom fusion | bytes 507968 | tf_op jit(solution)/shard_map/jit(_take)/gather | solution.py:96
  28.7 2.6 %fusion.70 = (bf16[1,16,48,512]{3,2,1,0:T(8,128)(2,1)}, bf16[1,16,48,512]{3,2,1,0:T(8,128)(2,1)}) fusion(bf16[2,16,48,512]{3,2,1,0:T(8,128)(2,1)} %param.16), kind=kLoop, calls=%fused_computation.138 | loop fusion | bytes 3145728 | tf_op jit(solution)/shard_map/slice | solution.py:130
  31.4 1.7 reshape_squeeze.6
  33.1 2.4 %reshape_squeeze.7 = bf16[16,48,4,128]{3,2,1,0:T(4,128)(2,1)} reshape(bf16[1,16,48,512]{3,2,1,0:T(8,128)(2,1)} %get-tuple-element.7) | data formatting | bytes 1572864 | tf_op jit(solution)/shard_map/reshape;squeeze | solution.py:131
  36.2 1.9 %fusion.42 = bf16[2,31,16,1,128]{4,0,1,3,2:T(2,128)(2,1)} fusion(bf16[16,2,31,128]{3,1,2,0:T(2,128)(2,1)} %gather_fusion.1, pred[16]{0:T(512)(128)(4,1)} %compare_and_fusion.1), kind=kLoop, calls=%fused_computation.61 | loop fusion | flops 126976 | bytes 507920 | tf_op jit(solution)/shard_map/jit(_take)/select_n | solution.py:96
  38.9 1.5 fusion.34
  40.4 7.3 %all-to-all-start.1 = ((bf16[2,31,16,1,128]{4,0,1,3,2:T(2,128)(2,1)}), bf16[2,31,16,1,128]{4,0,1,3,2:T(2,128)(2,1)}, u32[]{:S(2)}, u32[]{:S(2)}) async-start(bf16[2,31,16,1,128]{4,0,1,3,2:T(2,128)(2,1)} %fusion.42), calls=%async_computation.1 | async-start | bytes 507904 | tf_op jit(solution)/shard_map/all_to_all | solution.py:102
  48.4 1.5 convolution_bitcast_fusion.1
  51.0 1.1 pad_maximum_fusion
  52.1 7.0 %all-to-all-done.1 = bf16[2,31,16,1,128]{4,0,1,3,2:T(2,128)(2,1)} async-done(((bf16[2,31,16,1,128]{4,0,1,3,2:T(2,128)(2,1)}), bf16[2,31,16,1,128]{4,0,1,3,2:T(2,128)(2,1)}, u32[]{:S(2)}, u32[]{:S(2)}) %all-to-all-start.1) | async-done | bytes 253984 | tf_op jit(solution)/shard_map/all_to_all | solution.py:102
  59.1 3.5 %all-to-all-start.3 = ((f32[1,16,32,130]{3,1,0,2:T(8,128)}), f32[1,16,32,130]{3,1,0,2:T(8,128)S(1)}, u32[]{:S(2)}, u32[]{:S(2)}) async-start(f32[1,16,32,130]{3,1,0,2:T(8,128)} %pad_maximum_fusion), calls=%async_computation.3 | async-start | bytes 1048576 | tf_op jit(solution)/shard_map/all_to_all | solution.py:34
  64.5 2.8 %fusion.6 = (f32[496,2]{0,1:T(2,128)S(1)}, f32[2,496,496]{2,1,0:T(8,128)}) fusion(pred[496,496]{0,1:T(8,128)(4,1)S(1)} %copy-done.4, bf16[2,496,2,128]{3,1,2,0:T(8,128)(2,1)S(1)} %broadcast_select_fusion.2, bf16[496,256]{1,0:T(8,128)(2,1)} %param.11), kind=kOutput, calls=%fused_computation.15 | convolution fusion | flops 127435296 | bytes 2733952 | tf_op jit(solution)/shard_map/thd,phd->thp/dot_general | solution.py:47
  67.3 12.1 %all-to-all-done.3 = f32[1,16,32,130]{3,1,0,2:T(8,128)S(1)} async-done(((f32[1,16,32,130]{3,1,0,2:T(8,128)}), f32[1,16,32,130]{3,1,0,2:T(8,128)S(1)}, u32[]{:S(2)}, u32[]{:S(2)}) %all-to-all-start.3) | async-done | bytes 266272 | tf_op jit(solution)/shard_map/all_to_all | solution.py:34
  79.4 3.5 %all-to-all-start = ((bf16[2,64,16,1,128]{4,1,0,3,2:T(8,128)(2,1)}), bf16[2,64,16,1,128]{4,1,0,3,2:T(8,128)(2,1)S(1)}, u32[]{:S(2)}, u32[]{:S(2)}) async-start(bf16[2,64,16,1,128]{4,1,0,3,2:T(8,128)(2,1)} %fusion.34), calls=%async_computation | async-start | bytes 1048576 | tf_op jit(solution)/shard_map/all_to_all | solution.py:101
  83.1 2.6 %copy.139 = f32[1,16,16,2,130]{1,2,4,3,0:T(8,128)} copy(f32[1,16,16,2,130]{4,1,3,2,0:T(8,128)S(1)} %bitcast.193) | data formatting | bytes 532480 | tf_op jit(solution)/shard_map/all_to_all | solution.py:34
  88.1 2.1 %fusion.5 = f32[16,2,128]{0,2,1:T(8,128)S(1)} fusion(f32[16,16,2,130]{1,0,3,2:T(8,128)} %bitcast.191, f32[16,16,2]{1,0,2:T(8,128)S(1)} %exponential_bitcast_fusion), kind=kLoop, calls=%fused_computation.12 | loop fusion | flops 126976 | bytes 280576 | tf_op jit(solution)/shard_map/reduce_sum | solution.py:156
  90.6 8.9 %all-to-all-done = bf16[2,64,16,1,128]{4,1,0,3,2:T(8,128)(2,1)S(1)} async-done(((bf16[2,64,16,1,128]{4,1,0,3,2:T(8,128)(2,1)}), bf16[2,64,16,1,128]{4,1,0,3,2:T(8,128)(2,1)S(1)}, u32[]{:S(2)}, u32[]{:S(2)}) %all-to-all-start) | async-done | bytes 524320 | tf_op jit(solution)/shard_map/all_to_all | solution.py:101
  104.8 3.2 %convolution_convert_fusion = bf16[512,4096]{1,0:T(8,128)(2,1)} fusion(bf16[256,4096]{1,0:T(8,128)(2,1)S(1)} %copy-done, bf16[16,256]{0,1:T(8,128)(2,1)S(1)} %copy.147, bf16[496,256]{0,1:T(8,128)(2,1)S(1)} %bitcast.194), kind=kOutput, calls=%fused_computation.3 | convolution fusion | flops 1076363264 | bytes 6553600 | tf_op jit(solution)/shard_map/dot_general | solution.py:178
  108.0 62.4 %reduce-scatter.2.cloned.1.call-done = bf16[32,4096]{1,0:T(8,128)(2,1)} async-done(((bf16[512,4096]{1,0:T(8,128)(2,1)}), bf16[32,4096]{1,0:T(8,128)(2,1)}) %reduce-scatter.2.cloned.1.call-update) | async-done | bytes 262160 | tf_op jit(solution)/shard_map/reduce_scatter | solution.py:177
  170.4 1.1 multiply_reduce_fusion
  171.5 1.8 %multiply_convert_fusion = (bf16[32,4096]{1,0:T(8,128)(2,1)}, bf16[32,4096]{1,0:T(8,128)(2,1)}) fusion(bf16[32,4096]{1,0:T(8,128)(2,1)} %reduce-scatter.2.cloned.1.call-done, bf16[32,4096]{1,0:T(8,128)(2,1)S(1)} %copy-done.2, f32[4096]{0:T(1024)S(1)} %copy-done.9, f32[32]{0:T(128)S(1)} %add_rsqrt_fusion), kind=kLoop, calls=%fused_computation.45 | loop fusion | flops 917504 | bytes 1065088 | tf_op jit(solution)/shard_map/convert_element_type | solution.py:185
  (80 shorter events, 19.3 us)
Async XLA Ops:
  7.2 97.6 %copy-start = (bf16[256,4096]{1,0:T(8,128)(2,1)S(1)}, bf16[256,4096]{1,0:T(8,128)(2,1)}, u32[]{:S(2)}) copy-start(bf16[256,4096]{1,0:T(8,128)(2,1)} %param.19) | copy-start | bytes 6291460
  7.2 19.2 %copy-start.3 = (bf16[2,31,512]{2,0,1:T(2,128)(2,1)S(1)}, bf16[2,31,512]{2,0,1:T(2,128)(2,1)}, u32[]{:S(2)}) copy-start(bf16[2,31,512]{2,0,1:T(2,128)(2,1)} %param.12) | copy-start | bytes 190468
  8.7 31.7 %all-to-all-start.2 = ((bf16[16,16,256]{2,1,0:T(8,128)(2,1)}), bf16[16,16,256]{2,1,0:T(8,128)(2,1)S(1)}, u32[]{:S(2)}, u32[]{:S(2)}) async-start(bf16[16,16,256]{2,1,0:T(8,128)(2,1)} %broadcast_in_dim.154), calls=%async_computation.2 | async-start | bytes 262144 | tf_op jit(solution)/shard_map/all_to_all | solution.py:16
  40.4 18.8 %all-to-all-start.1 = ((bf16[2,31,16,1,128]{4,0,1,3,2:T(2,128)(2,1)}), bf16[2,31,16,1,128]{4,0,1,3,2:T(2,128)(2,1)}, u32[]{:S(2)}, u32[]{:S(2)}) async-start(bf16[2,31,16,1,128]{4,0,1,3,2:T(2,128)(2,1)} %fusion.42), calls=%async_computation.1 | async-start | bytes 507904 | tf_op jit(solution)/shard_map/all_to_all | solution.py:102
  49.9 13.7 %copy-start.12 = (pred[2]{0:T(512)(128)(4,1)S(1)}, pred[2]{0:T(512)(128)(4,1)}, u32[]{:S(2)}) copy-start(pred[2]{0:T(512)(128)(4,1)} %compare_and_fusion.2) | copy-start | bytes 10
  50.5 14.1 %copy-start.4 = (pred[496,496]{0,1:T(8,128)(4,1)S(1)}, pred[496,496]{0,1:T(8,128)(4,1)}, u32[]{:S(2)}) copy-start(pred[496,496]{0,1:T(8,128)(4,1)} %iota_compare_fusion) | copy-start | bytes 738052
  59.1 20.2 %all-to-all-start.3 = ((f32[1,16,32,130]{3,1,0,2:T(8,128)}), f32[1,16,32,130]{3,1,0,2:T(8,128)S(1)}, u32[]{:S(2)}, u32[]{:S(2)}) async-start(f32[1,16,32,130]{3,1,0,2:T(8,128)} %pad_maximum_fusion), calls=%async_computation.3 | async-start | bytes 1048576 | tf_op jit(solution)/shard_map/all_to_all | solution.py:34
  63.7 0.8 copy-start.5
  67.3 19.9 %copy-start.11 = (f32[16,2]{0,1:T(2,128)S(1)}, f32[16,2]{0,1:T(2,128)}, u32[]{:S(2)}) copy-start(f32[16,2]{0,1:T(2,128)} %fusion.53) | copy-start | bytes 388
  79.4 20.2 %all-to-all-start = ((bf16[2,64,16,1,128]{4,1,0,3,2:T(8,128)(2,1)}), bf16[2,64,16,1,128]{4,1,0,3,2:T(8,128)(2,1)S(1)}, u32[]{:S(2)}, u32[]{:S(2)}) async-start(bf16[2,64,16,1,128]{4,1,0,3,2:T(8,128)(2,1)} %fusion.34), calls=%async_computation | async-start | bytes 1048576 | tf_op jit(solution)/shard_map/all_to_all | solution.py:101
  82.9 87.5 %reduce-scatter.2.cloned.1.call-start = ((), (), s32[]{:S(2)}) async-start(), calls=%async_computation.5 | async-start | bytes 4456448 | tf_op jit(solution)/shard_map/reduce_scatter | solution.py:177
  83.1 7.3 %copy-start.8 = (f32[1,16,2,128]{3,2,1,0:T(2,128)S(1)}, f32[1,16,2,128]{3,2,1,0:T(2,128)}, u32[]{:S(2)}) copy-start(f32[1,16,2,128]{3,2,1,0:T(2,128)} %copy.145) | copy-start | bytes 49156
  88.1 11.7 %copy-start.7 = (bf16[496,256]{1,0:T(8,128)(2,1)S(1)}, bf16[496,256]{1,0:T(8,128)(2,1)}, u32[]{:S(2)}) copy-start(bf16[496,256]{1,0:T(8,128)(2,1)} %param.11) | copy-start | bytes 761860
  88.1 11.7 %copy-start.10 = (pred[1024]{0:T(1024)(128)(4,1)S(1)}, pred[1024]{0:T(1024)(128)(4,1)}, u32[]{:S(2)}) copy-start(pred[1024]{0:T(1024)(128)(4,1)} %iota_compare_fusion.1) | copy-start | bytes 3076
  100.6 1.6 copy-start.1
  102.7 1.0 copy-start.6
  108.0 62.4 %copy-start.2 = (bf16[32,4096]{1,0:T(8,128)(2,1)S(1)}, bf16[32,4096]{1,0:T(8,128)(2,1)}, u32[]{:S(2)}) copy-start(bf16[32,4096]{1,0:T(8,128)(2,1)} %param.20) | copy-start | bytes 786436
  108.0 63.6 %copy-start.9 = (f32[4096]{0:T(1024)S(1)}, f32[4096]{0:T(1024)}, u32[]{:S(2)}) copy-start(f32[4096]{0:T(1024)} %param.21) | copy-start | bytes 49156
Sparse Core Ops, SparseCore 0:
  108.1 62.2 reduce-scatter.1
where the time goes:
time: 182 us; the launch traced here: 180 us
  waiting for transfers between devices  90.4 us (50%)
  starting transfers between devices  24.6 us (14%)
  local copies, waits for them, and re-layouts  20.3 us (11%)
  other arithmetic  19.2 us (11%)
  between operations  15 us (8%)
  matrix products  10.8 us (6%)
    reduce_scatter x1, waiting for transfers between devices, per_device(): lax.psum_scatter(jnp.dot(attended, out_weight, preferred_element_type=jnp...  62.4 us
    all_to_all x1, waiting for transfers between devices, in_one_piece(): lax.all_to_all(both, axis, split_axis=split_dim, concat_axis=concat_dim,...  12.1 us
    all_to_all x1, starting transfers between devices, copy_for_each(): return lax.all_to_all(copies, axis, split_axis=0, concat_axis=0, tiled=True)  10.1 us
    all_to_all x1, waiting for transfers between devices, per_device(): lax.all_to_all(spread(history_cache), 'tp', split_axis=2, concat_axis=1,...  8.93 us
    all_to_all x1, starting transfers between devices, per_device(): lax.all_to_all(spread(prompt_entries), 'tp', split_axis=2, concat_axis=1,...  7.27 us
    all_to_all x1, waiting for transfers between devices, per_device(): lax.all_to_all(spread(prompt_entries), 'tp', split_axis=2, concat_axis=1,...  7 us
  transfers between devices with their start and end apart: 5, of which 4 were waited for; matrix products, arithmetic and copies ran while one was open for 20% of the time, Pallas kernels for 0%

commit v1 on v0

v1 whole, which is shorter than its diff:
```python
import jax
import jax.numpy as jnp
from jax import lax
from jax.experimental import pallas as pl
from jax.experimental.pallas import tpu as pltpu
from jax.sharding import PartitionSpec as P

HEAD_DIM = 128
CHIPS = 8
GROUP = 16
SUBS = 4
MESH = pl.DeviceIdType.MESH
LOWEST = -(2.0**100)
FACTOR = HEAD_DIM**-0.5 * 1.4426950408889634
NEVER = 1 << 20

f32 = jnp.float32
bf16 = jnp.bfloat16


def dot_t(a, b):
    return lax.dot_general(a, b, (((1,), (1,)), ((), ())), preferred_element_type=f32)


def iota(shape, dim):
    return lax.broadcasted_iota(jnp.int32, shape, dim)


def kernel(
    start_ref, lengths_ref, pq, pe, hist, dq, de, dc, w, res, gain,
    out_res, out_norm,
    stage, pbuf, kv, qbuf, dbuf, qd, wbuf, resbuf, gainbuf, fresh,
    part_send, part_recv, part_mine, dec_send, dec_recv, att, rs_send, rs_recv, hid,
    local_sem, qd_ssem, qd_rsem, kv_ssem, kv_rsem, pair_ssem, pair_rsem,
    part_ssem, part_rsem, dec_ssem, dec_rsem, rs_ssem, rs_rsem,
):
    t = lax.axis_index("tp")
    y = t // 2
    c = t % 2
    head = y // 2
    half = y // 4
    partner = 2 * y + 1 - c
    span = hist.shape[1]
    rows = pq.shape[0]
    width = rs_send.shape[-1]

    def local(src, dst, n):
        return pltpu.make_async_copy(src, dst, local_sem.at[n])

    def remote(src, dst, ssem, rsem, device):
        return pltpu.make_async_remote_copy(
            src_ref=src, dst_ref=dst, send_sem=ssem, recv_sem=rsem,
            device_id={"tp": device}, device_id_type=MESH,
        )

    def lanes(index, size):
        return pl.ds(pl.multiple_of(index * size, size), size)

    locals_ = [
        local(hist, stage.at[:, pl.ds(0, span), :], 0),
        local(pe, pbuf, 1),
        local(hist.at[:, :, lanes(head, 128)], kv.at[:, y, pl.ds(0, span), :], 2),
        local(dc.at[:, :, :, lanes(c, 256)], dbuf.at[c], 3),
    ]
    for i in range(2):
        columns = pl.ds(128 * i, 128)
        locals_.append(local(pq.at[:, columns], qbuf.at[2 * c + i, pl.ds(0, rows), :], 4 + i))
        locals_.append(local(dq.at[:, columns], qbuf.at[2 * c + i, pl.ds(rows, 16), :], 6 + i))
    locals_ += [
        local(de.at[:, :, lanes(head, 128)], fresh, 8),
        local(w, wbuf.at[pl.ds(pl.multiple_of(256 * c, 256), 256), :], 9),
        local(res, resbuf, 10),
        local(gain, gainbuf, 11),
    ]
    for copy in locals_:
        copy.start()

    barrier = pltpu.get_barrier_semaphore()
    for k in range(1, GROUP):
        pl.semaphore_signal(
            barrier, inc=1, device_id={"tp": (t + k) % GROUP}, device_id_type=MESH
        )

    locals_[0].wait()
    locals_[1].wait()
    entries = pe.shape[1]
    for i in range(2):
        stage[i, span : span + 32, :] = jnp.concatenate(
            [pbuf[i], jnp.zeros((32 - entries, pbuf.shape[2]), bf16)], axis=0
        )
    for i in range(2):
        kv[i, y, span : span + 32, :] = stage[i, span : span + 32, lanes(head, 128)]
    rs_recv[0, 0, 2:4] = jnp.zeros((2, 32, width), bf16)
    rs_recv[1, 0, 0:2] = jnp.zeros((2, 32, width), bf16)
    pl.semaphore_wait(barrier, GROUP - 1)

    slot = t - 8 * half
    qd_copies = []
    for k in range(1, CHIPS):
        copy = remote(dq, qd.at[slot], qd_ssem.at[k], qd_rsem.at[slot], 2 * ((y + k) % CHIPS) + half)
        copy.start()
        qd_copies.append(copy)
    qd_pair = remote(dq, qd.at[slot], qd_ssem.at[0], qd_rsem.at[slot], partner)
    qd_own = pltpu.make_async_copy(dq, qd.at[slot], qd_rsem.at[slot])

    @pl.when(c == half)
    def _():
        qd_own.start()

    @pl.when(c != half)
    def _():
        qd_pair.start()

    kv_copies = []
    for k in (4, 3, 5, 2, 6, 1, 7):
        there = (y + k) % CHIPS
        copy = remote(
            stage.at[:, :, lanes(there // 2, 128)], kv.at[:, y], kv_ssem.at[k], kv_rsem.at[y],
            2 * there + c,
        )
        copy.start()
        kv_copies.append(copy)

    pairs = [remote(dc.at[:, :, :, lanes(1 - c, 256)], dbuf.at[c], pair_ssem.at[0], pair_rsem.at[0], partner)]
    for i in range(2):
        columns = pl.ds(128 * i, 128)
        pairs.append(
            remote(pq.at[:, columns], qbuf.at[2 * c + i, pl.ds(0, rows), :],
                   pair_ssem.at[1 + i], pair_rsem.at[1 + i], partner)
        )
        pairs.append(
            remote(dq.at[:, columns], qbuf.at[2 * c + i, pl.ds(rows, 16), :],
                   pair_ssem.at[3 + i], pair_rsem.at[3 + i], partner)
        )
    pairs.append(
        remote(w, wbuf.at[pl.ds(pl.multiple_of(256 * c, 256), 256), :],
               pair_ssem.at[5], pair_rsem.at[5], partner)
    )
    for copy in pairs:
        copy.start()

    row_b = iota((128, 1), 0) & 15
    limit = jnp.zeros((128, 1), jnp.int32)
    for b in range(16):
        limit = jnp.where(row_b == b, lengths_ref[b], limit)
    col = iota((1, 768), 1)
    col_b = (col * 1366) >> 16
    col_p = col - 48 * col_b
    lane = iota((128, 128), 1)

    locals_[3].wait()
    pairs[0].wait_recv()
    for s in range(8):
        pltpu.make_async_copy(dq, qd.at[s], qd_rsem.at[s]).wait()
    for g in range(2):
        columns = slice(128 * g, 128 * g + 128)
        q = jnp.concatenate(
            [qd[4 * g + n, :, 128 * i : 128 * i + 128] for n in range(4) for i in range(2)], axis=0
        )
        scores = []
        for core in range(2):
            keys = dbuf[core, 0, :, :, columns].reshape(768, 128)
            places = (2 * y + core) * 48 + col_p
            valid = (col_b == row_b) & (places < limit)
            scores.append(jnp.where(valid, dot_t(q, keys), LOWEST))
        top = jnp.maximum(*[jnp.max(s, axis=1, keepdims=True) for s in scores])
        top = top.astype(bf16).astype(f32)
        total = jnp.zeros((128, 1), f32)
        summed = jnp.zeros((128, 128), f32)
        for core in range(2):
            weights = jnp.exp2((scores[core] - top) * FACTOR)
            total += jnp.sum(weights, axis=1, keepdims=True)
            values = dbuf[core, 1, :, :, columns].reshape(768, 128)
            summed += jnp.dot(weights.astype(bf16), values, preferred_element_type=f32)
        stats = jnp.where(lane < 64, top, total).astype(bf16)
        summed = summed.astype(bf16)
        for n in range(2):
            dec_send[2 * g + n, 0] = summed[64 * n : 64 * n + 64]
            dec_send[2 * g + n, 1] = stats[64 * n : 64 * n + 64]
    dec_copies = []
    for j in range(4):
        copy = remote(dec_send.at[j], dec_recv.at[y], dec_ssem.at[j], dec_rsem.at[y], 2 * (4 * c + j) + 1)
        dec_copies.append(copy)
        stays = (c == 1) & (y == 4 + j)

        @pl.when(stays)
        def _():
            dec_recv[y] = dec_send[j]

        @pl.when(jnp.logical_not(stays))
        def _():
            copy.start()

    block = (col * 683) >> 16
    place = col - 96 * block
    owner = 2 * block + c
    start = start_ref[0]
    from_history = jnp.where(owner * span + place < start, -1, NEVER)
    from_prompt = jnp.where(place < span + entries, owner * entries + place - span, NEVER)
    first_row = jnp.where(place < span, from_history, from_prompt)
    row32 = iota((128, 1), 0) & 31

    for n in (2, 4, 5, 6, 7):
        locals_[n].wait()
    for copy in pairs[1:5]:
        copy.wait_recv()
    for k in range(1, CHIPS):
        there = (y + k) % CHIPS
        pltpu.make_async_copy(kv.at[:, there], kv.at[:, there], kv_rsem.at[there]).wait()

    def attend(row):
        row = pl.multiple_of(row, 32)
        q = qbuf[:, pl.ds(row, 32), :].reshape(128, 128)
        keys = kv[0].reshape(768, 128)
        values = kv[1].reshape(768, 128)
        scores = jnp.where(first_row <= row + row32, dot_t(q, keys), LOWEST)
        top = jnp.max(scores, axis=1, keepdims=True)
        weights = jnp.exp2((scores - top) * FACTOR)
        total = jnp.sum(weights, axis=1, keepdims=True)
        summed = jnp.dot(weights.astype(bf16), values, preferred_element_type=f32)
        return summed, jnp.where(lane < 64, top, total)

    def part_copy(i):
        return remote(part_send.at[i], part_recv.at[i], part_ssem.at[i], part_rsem.at[i], partner)

    def attend_both(i, d, slot):
        summed, stats = attend(64 * d + 32 * (1 - c))
        part_send[i, 0] = summed
        part_send[i, 1] = stats
        part_copy(i).start()
        summed, stats = attend(64 * d + 32 * c)
        part_mine[slot, 0] = summed
        part_mine[slot, 1] = stats

    def decode_rows(slot):
        for s in range(CHIPS):
            @pl.when(jnp.logical_not((y == s) & (y >= 4)))
            def _():
                pltpu.make_async_copy(dec_send.at[0], dec_recv.at[s], dec_rsem.at[s]).wait()
        query = qbuf[:, rows : rows + 16, :].astype(f32)
        key = fresh[0].astype(f32)
        value = fresh[1].astype(f32)
        own = jnp.sum(query * key[None], axis=-1, keepdims=True).reshape(64, 1)
        value = jnp.concatenate([value] * 4, axis=0)
        tops = [dec_recv[s, 1, :, 0:1].astype(f32) for s in range(CHIPS)]
        top = own
        for s in range(CHIPS):
            top = jnp.maximum(top, tops[s])
        own_weight = jnp.exp2((own - top) * FACTOR)
        total = own_weight
        summed = own_weight.astype(bf16).astype(f32) * value
        for s in range(CHIPS):
            factor = jnp.exp2((tops[s] - top) * FACTOR)
            total += factor * dec_recv[s, 1, :, 64:65].astype(f32)
            summed += factor * dec_recv[s, 0].astype(f32)
        out = (summed / total).astype(bf16)
        for n in range(4):
            att[slot, 16:32, 128 * n : 128 * n + 128] = out[16 * n : 16 * n + 16]

    def combine(i, d, slot):
        part_copy(i).wait_recv()
        mine, theirs = part_mine[slot, 1], part_recv[i, 1]
        top0, top1 = mine[:, 0:1], theirs[:, 0:1]
        top = jnp.maximum(top0, top1)
        factor0 = jnp.exp2((top0 - top) * FACTOR)
        factor1 = jnp.exp2((top1 - top) * FACTOR)
        total = factor0 * mine[:, 64:65] + factor1 * theirs[:, 64:65]
        out = (factor0 * part_mine[slot, 0] + factor1 * part_recv[i, 0]) / total
        out = out.astype(bf16)
        for n in range(4):
            att[slot, :, 128 * n : 128 * n + 128] = out[32 * n : 32 * n + 32]

        @pl.when((d == CHIPS - 1) & (c == 1))
        def _():
            decode_rows(slot)

    def project(slot, sub):
        return jnp.dot(att[slot], wbuf[:, lanes(sub, width)], preferred_element_type=f32)

    right, left = 2 * ((y + 1) % CHIPS) + c, 2 * ((y + 7) % CHIPS) + c

    def rs_copy(way, step, sub):
        return remote(
            rs_send.at[way, step, sub], rs_recv.at[way, step, sub],
            rs_ssem.at[way, step, sub], rs_rsem.at[way, step, sub], right if way == 0 else left,
        )

    far = (y + 4) % CHIPS
    attend_both(0, far, 0)
    locals_[8].wait()
    locals_[9].wait()
    pairs[5].wait_recv()
    combine(0, far, 0)
    for j in range(2):
        for way in range(2):
            sub = j + 2 * way
            rs_send[way, 0, sub] = project(0, sub).astype(bf16)
            rs_copy(way, 0, sub).start()

    def step_body(step, carry):
        away = 4 - step
        ahead, behind = (y + away) % CHIPS, (y + CHIPS - away) % CHIPS
        def both(j, carry):
            attend_both(2 * step - 1 + j, jnp.where(j == 0, ahead, behind), j)
            return carry
        lax.fori_loop(0, 2, both, 0)
        def join(j, carry):
            combine(2 * step - 1 + j, jnp.where(j == 0, ahead, behind), j)
            return carry
        lax.fori_loop(0, 2, join, 0)

        def sub_body(j, carry):
            for way in range(2):
                sub = (j + 2) % SUBS if way == 0 else j
                own = project(way, sub)

                @pl.when((step > 1) | (j >= 2))
                def _():
                    rs_copy(way, step - 1, sub).wait_recv()

                rs_send[way, step, sub] = (own + rs_recv[way, step - 1, sub].astype(f32)).astype(bf16)
                rs_copy(way, step, sub).start()
            return carry
        return lax.fori_loop(0, SUBS, sub_body, carry)

    lax.fori_loop(1, 4, step_body, 0)

    attend_both(7, y, 0)
    combine(7, y, 0)
    locals_[10].wait()
    locals_[11].wait()

    def own_body(sub, carry):
        hid[:, lanes(sub, width)] = project(0, sub) + resbuf[:, lanes(sub, width)].astype(f32)
        return carry
    lax.fori_loop(0, SUBS, own_body, 0)

    def last_body(j, squares):
        for way in range(2):
            sub = (j + 2) % SUBS if way == 0 else j
            rs_copy(way, 3, sub).wait_recv()
            hid[:, lanes(sub, width)] += rs_recv[way, 3, sub].astype(f32)
        return squares
    lax.fori_loop(0, SUBS, last_body, 0)

    hidden = hid[...]
    out_res[...] = hidden.astype(bf16)
    mean_square = jnp.sum(hidden * hidden, axis=1, keepdims=True) * (1.0 / hidden.shape[1])
    out_norm[...] = (hidden * lax.rsqrt(mean_square + 1e-05) * gainbuf[...]).astype(bf16)

    for copy in qd_copies + kv_copies + pairs:
        copy.wait_send()

    @pl.when(c != half)
    def _():
        qd_pair.wait_send()

    for j in range(4):
        @pl.when(jnp.logical_not((c == 1) & (y == 4 + j)))
        def _():
            dec_copies[j].wait_send()

    def part_done(i, carry):
        part_copy(i).wait_send()
        return carry
    lax.fori_loop(0, 8, part_done, 0)
    for j in range(2):
        for way in range(2):
            rs_copy(way, 0, j + 2 * way).wait_send()

    def rs_done(n, carry):
        for way in range(2):
            rs_copy(way, 1 + n // SUBS, n % SUBS).wait_send()
        return carry
    lax.fori_loop(0, 3 * SUBS, rs_done, 0)


def per_device(
    prompt_queries, prompt_entries, history_cache, decode_queries, decode_entries, decode_cache,
    decode_lengths, prompt_start, out_weight, residual, norm_gain,
):
    hbm = pl.BlockSpec(memory_space=pltpu.HBM)
    smem = pl.BlockSpec(memory_space=pltpu.SMEM)
    vmem = pl.BlockSpec(memory_space=pltpu.VMEM)
    span = history_cache.shape[1]
    tokens, width = residual.shape
    dma = pltpu.SemaphoreType.DMA
    shape = jax.ShapeDtypeStruct(residual.shape, residual.dtype)
    return pl.pallas_call(
        kernel,
        out_shape=(shape, shape),
        in_specs=[smem, smem] + [hbm] * 9,
        out_specs=(vmem, vmem),
        scratch_shapes=[
            pltpu.VMEM((2, span + 32, 512), bf16),
            pltpu.VMEM(prompt_entries.shape, bf16),
            pltpu.VMEM((2, CHIPS, span + 32, 128), bf16),
            pltpu.VMEM((4, 512, 128), bf16),
            pltpu.VMEM((2, 2, 16, 48, 256), bf16),
            pltpu.VMEM((8, 16, 256), bf16),
            pltpu.VMEM((512, width), bf16),
            pltpu.VMEM((tokens, width), bf16),
            pltpu.VMEM((1, width), f32),
            pltpu.VMEM((2, 16, 128), bf16),
            pltpu.VMEM((8, 2, 128, 128), f32),
            pltpu.VMEM((8, 2, 128, 128), f32),
            pltpu.VMEM((2, 2, 128, 128), f32),
            pltpu.VMEM((4, 2, 64, 128), bf16),
            pltpu.VMEM((CHIPS, 2, 64, 128), bf16),
            pltpu.VMEM((2, 32, 512), bf16),
            pltpu.VMEM((2, 4, SUBS, 32, width // SUBS), bf16),
            pltpu.VMEM((2, 4, SUBS, 32, width // SUBS), bf16),
            pltpu.VMEM((tokens, width), f32),
            dma((12,)), dma((8,)), dma((8,)), dma((8,)), dma((8,)), dma((6,)), dma((6,)),
            dma((8,)), dma((8,)), dma((4,)), dma((8,)), dma((2, 4, SUBS)), dma((2, 4, SUBS)),
        ],
        compiler_params=pltpu.CompilerParams(collective_id=0, has_side_effects=True),
    )(
        prompt_start, decode_lengths, prompt_queries, prompt_entries, history_cache, decode_queries,
        decode_entries, decode_cache, out_weight, residual, norm_gain.reshape(1, -1),
    )


def solution(mesh):
    placed = (
        P("rep", "tp"),
        P("rep", "tp", None),
        P("rep", "tp", None),
        P("rep", "tp"),
        P("rep", None, None),
        P("rep", None, "tp", None),
        P("rep"),
        P("rep"),
        P("tp", None),
        P("tp", "rep"),
        P(None),
    )
    return jax.shard_map(
        per_device, mesh=mesh, in_specs=placed, out_specs=(P("tp", "rep"), P("tp", "rep")),
        check_vma=False,
    )
```

time: 182 us -> 57.5 us (0.32)
  waiting for transfers between devices: 90.4 us -> 0 us
  Pallas kernels: 0 us -> 51.2 us
  starting transfers between devices: 24.6 us -> 0 us
  other arithmetic: 19.2 us -> 0 us
  local copies, waits for them, and re-layouts: 20.3 us -> 4.81 us
  between operations: 15 us -> 1.29 us
  matrix products: 10.8 us -> 0 us
    reduce_scatter x1 -> x0, waiting for transfers between devices: 62.4 us -> none  [per_device(): lax.psum_scatter(jnp.dot(attended, out_weight, preferred_element_type=jnp...]
    pallas_call x0 -> x1, Pallas kernels: none -> 51.2 us  [per_device(): pl.pallas_call(kernel, out_shape=(shape, shape), in_specs=[smem, smem] +...]
    all_to_all x4 -> x0, waiting for transfers between devices: 28 us -> none  [the longest x1 12.1 us: in_one_piece(): lax.all_to_all(both, axis, split_axis=split_dim, concat_axis=concat_dim,...]
    all_to_all x4 -> x0, starting transfers between devices: 24.3 us -> none  [the longest x1 10.1 us: copy_for_each(): return lax.all_to_all(copies, axis, split_axis=0, concat_axis=0, tiled=True)]
    dot_general x7 -> x0, matrix products: 10.8 us -> none  [the longest x2 3.58 us: absorb(): jnp.einsum('thd,phd->thp', queries, keys, preferred_element_type=jnp.floa...]
    reduce_sum x7 -> x0, other arithmetic: 7.17 us -> none  [the longest x1 2.09 us: per_device(): summed_heads = jnp.sum(parts_summed * factor[..., None], axis=0)]
    another operation x6 -> x0, local copies, waits for them, and re-layouts: 4.92 us -> none  [the longest x1 2.44 us: per_device(): decode_cache[1].reshape(decode_rows, span, KV_HEADS, HEAD_DIM)]
    gather x4 -> x0, local copies, waits for them, and re-layouts: 4.08 us -> none  [the longest x2 2.54 us: spread(): jnp.take(shaped, targets.reshape(-1), axis=2)]
  transfers between devices with their start and end apart: 5 -> 0, of which waited for: 4 -> 0; matrix products, arithmetic and copies ran while one was open for 20% -> 0% of each run, Pallas kernels for 0% -> 0%
where the time goes in v1:
time: 57.5 us; the launch traced here: 57.3 us
  Pallas kernels  51.2 us (89%)
  local copies, waits for them, and re-layouts  4.81 us (8%)
  between operations  1.29 us (2%)
    pallas_call x1, Pallas kernels, per_device(): pl.pallas_call(kernel, out_shape=(shape, shape), in_specs=[smem, smem] +...  51.2 us
    unnamed x3, local copies, waits for them, and re-layouts  4.81 us

profile of v1, /device:TPU:1, one launch (start us, length us, event | category | flops | bytes accessed | tf_op | source)
XLA Modules:
  0.0 57.3 jit_solution(3927261291067175016)
XLA Ops:
  1.3 1.5 %copy.13.pe = bf16[2,31,512]{2,1,0:T(8,128)(2,1)} copy(bf16[2,31,512]{2,0,1:T(2,128)(2,1)} %param.12) | data formatting | bytes 126976 | tf_op args[1]
  2.7 51.2 %shard_map.122 = (bf16[32,4096]{1,0:T(8,128)(2,1)}, bf16[32,4096]{1,0:T(8,128)(2,1)}) custom-call(s32[1]{0:T(128)S(6)} %copy.16.start_ref, s32[16]{0:T(128)} %lengths_ref.1, bf16[496,256]{1,0:T(8,128)(2,1)} %pq.1, bf16[2,31,512]{2,1,0:T(8,128)(2,1)} %copy.13.pe, bf16[2,64,512]{2,1,0:T(8,128)(2,1)} %hist.1, bf16[16,256]{1,0:T(8,128)(2,1)} %dq.1, ...), custom_call_target="tpu_custom_call" | custom-call | tf_op jit(solution)/shard_map/pallas_call | solution.py:389
  53.9 1.7 %copy.17 = bf16[32,4096]{1,0:T(8,128)(2,1)} copy(bf16[32,4096]{1,0:T(8,128)(2,1)} %get-tuple-element.4) | data formatting | bytes 524288
  55.6 1.7 %copy.18 = bf16[32,4096]{1,0:T(8,128)(2,1)} copy(bf16[32,4096]{1,0:T(8,128)(2,1)} %get-tuple-element.5) | data formatting | bytes 524288

commit v2 on v1

v2 whole, which is shorter than its diff:
```python
import jax
import jax.numpy as jnp
from jax import lax
from jax.experimental import pallas as pl
from jax.experimental.pallas import tpu as pltpu
from jax.sharding import PartitionSpec as P

HEAD_DIM = 128
CHIPS = 8
GROUP = 16
SUBS = 4
MESH = pl.DeviceIdType.MESH
LOWEST = -(2.0**100)
FACTOR = HEAD_DIM**-0.5 * 1.4426950408889634
NEVER = 1 << 20

f32 = jnp.float32
bf16 = jnp.bfloat16


def dot_t(a, b):
    return lax.dot_general(a, b, (((1,), (1,)), ((), ())), preferred_element_type=f32)


def iota(shape, dim):
    return lax.broadcasted_iota(jnp.int32, shape, dim)


def kernel(
    start_in, lengths_in, pq, pe, hist, dq, de, dc, w, res,
    hid,
    start_ref, lengths_ref, stage, pbuf, kv, qbuf, dbuf, qd, wbuf, resbuf, fresh,
    dec_send, dec_recv, att, own, rs_send, rs_recv,
    local_sem, qd_ssem, qd_rsem, kv_ssem, kv_rsem, pair_ssem, pair_rsem,
    dec_ssem, dec_rsem, rs_ssem, rs_rsem,
):
    t = lax.axis_index("tp")
    y = t // 2
    c = t % 2
    head = y // 2
    half = y // 4
    partner = 2 * y + 1 - c
    outward = 2 * (y % 2) - 1
    span = hist.shape[1]
    entries = pe.shape[0]
    rows = pq.shape[0]
    width = rs_send.shape[-1]

    def chip(steps):
        return (y + outward * steps + CHIPS) % CHIPS

    def local(src, dst, n):
        return pltpu.make_async_copy(src, dst, local_sem.at[n])

    def remote(src, dst, ssem, rsem, device):
        return pltpu.make_async_remote_copy(
            src_ref=src, dst_ref=dst, send_sem=ssem, recv_sem=rsem,
            device_id={"tp": device}, device_id_type=MESH,
        )

    def lanes(index, size):
        return pl.ds(pl.multiple_of(index * size, size), size)

    locals_ = [
        local(hist, stage.at[:, pl.ds(0, span), :], 0),
        local(pe, pbuf, 1),
        local(hist.at[:, :, lanes(head, 128)], kv.at[:, t, pl.ds(0, span), :], 2),
        local(dc.at[:, :, :, lanes(c, 256)], dbuf.at[c], 3),
    ]
    for i in range(2):
        columns = pl.ds(128 * i, 128)
        locals_.append(local(pq.at[:, columns], qbuf.at[2 * c + i, pl.ds(0, rows), :], 4 + i))
        locals_.append(local(dq.at[:, columns], qbuf.at[2 * c + i, pl.ds(rows, 16), :], 6 + i))
    locals_ += [
        local(de.at[:, :, lanes(head, 128)], fresh, 8),
        local(w, wbuf.at[pl.ds(pl.multiple_of(256 * c, 256), 256), :], 9),
        local(res, resbuf, 10),
        local(start_in, start_ref, 11),
        local(lengths_in, lengths_ref, 12),
    ]
    for copy in locals_:
        copy.start()

    barrier = pltpu.get_barrier_semaphore()
    for k in range(1, GROUP):
        pl.semaphore_signal(
            barrier, inc=1, device_id={"tp": (t + k) % GROUP}, device_id_type=MESH
        )

    locals_[0].wait()
    locals_[1].wait()
    for i in range(2):
        stage[i, span : span + 32, :] = jnp.concatenate(
            [pbuf[:, i, :], jnp.zeros((32 - entries, pbuf.shape[2]), bf16)], axis=0
        )
    for i in range(2):
        kv[i, t, span : span + 32, :] = stage[i, span : span + 32, lanes(head, 128)]
    rs_recv[0, 0, 2:4] = jnp.zeros((2, 32, width), bf16)
    rs_recv[1, 0, 0:2] = jnp.zeros((2, 32, width), bf16)
    pl.semaphore_wait(barrier, GROUP - 1)

    place = t - 8 * half
    qd_copies = []
    for k in range(1, CHIPS):
        copy = remote(dq, qd.at[place], qd_ssem.at[k], qd_rsem.at[place], 2 * ((y + k) % CHIPS) + half)
        copy.start()
        qd_copies.append(copy)
    qd_pair = remote(dq, qd.at[place], qd_ssem.at[0], qd_rsem.at[place], partner)
    qd_own = pltpu.make_async_copy(dq, qd.at[place], qd_rsem.at[place])

    @pl.when(c == half)
    def _():
        qd_own.start()

    @pl.when(c != half)
    def _():
        qd_pair.start()

    kv_copies = []

    def send_kv(src, slot, device):
        n = len(kv_copies)
        copy = remote(src, kv.at[:, slot], kv_ssem.at[n], kv_rsem.at[slot], device)
        copy.start()
        kv_copies.append(copy)

    def own_block(there):
        return stage.at[:, :, lanes(there // 2, 128)]

    mate = chip(-1)
    for steps in (3, -2, 1, -1):
        there = chip(steps)
        send_kv(own_block(there), t, 2 * there + c)

    pairs = [remote(dc.at[:, :, :, lanes(1 - c, 256)], dbuf.at[c], pair_ssem.at[0], pair_rsem.at[0], partner)]
    for i in range(2):
        columns = pl.ds(128 * i, 128)
        pairs.append(
            remote(pq.at[:, columns], qbuf.at[2 * c + i, pl.ds(0, rows), :],
                   pair_ssem.at[1 + i], pair_rsem.at[1 + i], partner)
        )
        pairs.append(
            remote(dq.at[:, columns], qbuf.at[2 * c + i, pl.ds(rows, 16), :],
                   pair_ssem.at[3 + i], pair_rsem.at[3 + i], partner)
        )
    pairs.append(
        remote(w, wbuf.at[pl.ds(pl.multiple_of(256 * c, 256), 256), :],
               pair_ssem.at[5], pair_rsem.at[5], partner)
    )
    for copy in pairs:
        copy.start()
    send_kv(own_block(y), t, partner)

    def wait_kv(slot):
        pltpu.make_async_copy(kv.at[:, slot], kv.at[:, slot], kv_rsem.at[slot]).wait()

    for steps in (2, 1, 3):
        slot = 2 * chip(steps) + c
        wait_kv(slot)
        send_kv(kv.at[:, slot], slot, 2 * mate + c)
        send_kv(kv.at[:, slot], slot, partner)

    locals_[11].wait()
    locals_[12].wait()
    row_b = iota((128, 1), 0) & 15
    limit = jnp.zeros((128, 1), jnp.int32)
    for b in range(16):
        limit = jnp.where(row_b == b, lengths_ref[b], limit)
    col = iota((1, 768), 1)
    col_b = (col * 1366) >> 16
    col_p = col - 48 * col_b
    lane = iota((128, 128), 1)

    locals_[3].wait()
    pairs[0].wait_recv()
    for s in range(8):
        pltpu.make_async_copy(dq, qd.at[s], qd_rsem.at[s]).wait()
    for g in range(2):
        columns = slice(128 * g, 128 * g + 128)
        q = jnp.concatenate(
            [qd[4 * g + n, :, 128 * i : 128 * i + 128] for n in range(4) for i in range(2)], axis=0
        )
        scores = []
        for core in range(2):
            keys = dbuf[core, 0, :, :, columns].reshape(768, 128)
            places = (2 * y + core) * 48 + col_p
            valid = (col_b == row_b) & (places < limit)
            scores.append(jnp.where(valid, dot_t(q, keys), LOWEST))
        top = jnp.maximum(*[jnp.max(s, axis=1, keepdims=True) for s in scores])
        top = top.astype(bf16).astype(f32)
        total = jnp.zeros((128, 1), f32)
        summed = jnp.zeros((128, 128), f32)
        for core in range(2):
            weights = jnp.exp2((scores[core] - top) * FACTOR)
            total += jnp.sum(weights, axis=1, keepdims=True)
            values = dbuf[core, 1, :, :, columns].reshape(768, 128)
            summed += jnp.dot(weights.astype(bf16), values, preferred_element_type=f32)
        stats = jnp.where(lane < 64, top, total).astype(bf16)
        summed = summed.astype(bf16)
        for n in range(2):
            dec_send[2 * g + n, 0] = summed[64 * n : 64 * n + 64]
            dec_send[2 * g + n, 1] = stats[64 * n : 64 * n + 64]
    dec_copies = []
    for j in range(4):
        copy = remote(dec_send.at[j], dec_recv.at[y], dec_ssem.at[j], dec_rsem.at[y], 2 * (4 * c + j) + 1)
        dec_copies.append(copy)
        stays = (c == 1) & (y == 4 + j)

        @pl.when(stays)
        def _():
            dec_recv[y] = dec_send[j]

        @pl.when(jnp.logical_not(stays))
        def _():
            copy.start()

    for steps in (-1, -3, -2, -4):
        slot = 2 * chip(steps) + c
        wait_kv(slot)
        send_kv(kv.at[:, slot], slot, partner)
    col = iota((1, 1536), 1)
    owner = (col * 683) >> 16
    place = col - 96 * owner
    start = start_ref[0]
    from_history = jnp.where(owner * span + place < start, -1, NEVER)
    from_prompt = jnp.where(place < span + entries, owner * entries + place - span, NEVER)
    first_row = jnp.where(place < span, from_history, from_prompt)
    row32 = iota((128, 1), 0) & 31

    for n in (2, 4, 5, 6, 7):
        locals_[n].wait()
    for copy in pairs[1:5]:
        copy.wait_recv()
    for k in range(CHIPS):
        wait_kv(2 * ((y + k) % CHIPS) + 1 - c)

    def decode_rows(slot):
        for s in range(CHIPS):
            @pl.when(jnp.logical_not((y == s) & (y >= 4)))
            def _():
                pltpu.make_async_copy(dec_send.at[0], dec_recv.at[s], dec_rsem.at[s]).wait()
        query = qbuf[:, rows : rows + 16, :].astype(f32)
        key = fresh[0].astype(f32)
        value = fresh[1].astype(f32)
        own = jnp.sum(query * key[None], axis=-1, keepdims=True).reshape(64, 1)
        value = jnp.concatenate([value] * 4, axis=0)
        tops = [dec_recv[s, 1, :, 0:1].astype(f32) for s in range(CHIPS)]
        top = own
        for s in range(CHIPS):
            top = jnp.maximum(top, tops[s])
        own_weight = jnp.exp2((own - top) * FACTOR)
        total = own_weight
        summed = own_weight.astype(bf16).astype(f32) * value
        for s in range(CHIPS):
            factor = jnp.exp2((tops[s] - top) * FACTOR)
            total += factor * dec_recv[s, 1, :, 64:65].astype(f32)
            summed += factor * dec_recv[s, 0].astype(f32)
        out = (summed / total).astype(bf16)
        for n in range(4):
            att[slot, 16:32, 128 * n : 128 * n + 128] = out[16 * n : 16 * n + 16]

    def attend(d, slot):
        row = pl.multiple_of(64 * d + 32 * c, 32)
        q = qbuf[:, pl.ds(row, 32), :].reshape(128, 128)
        keys = kv[0].reshape(1536, 128)
        values = kv[1].reshape(1536, 128)
        scores = jnp.where(first_row <= row + row32, dot_t(q, keys), LOWEST)
        top = jnp.max(scores, axis=1, keepdims=True)
        weights = jnp.exp2((scores - top) * FACTOR)
        total = jnp.sum(weights, axis=1, keepdims=True)
        summed = jnp.dot(weights.astype(bf16), values, preferred_element_type=f32)
        out = (summed / total).astype(bf16)
        for n in range(4):
            att[slot, :, 128 * n : 128 * n + 128] = out[32 * n : 32 * n + 32]

        @pl.when((d == CHIPS - 1) & (c == 1))
        def _():
            decode_rows(slot)

    def project(sub):
        return jnp.dot(att[0], wbuf[:, lanes(sub, width)], preferred_element_type=f32)

    right, left = 2 * ((y + 1) % CHIPS) + c, 2 * ((y + 7) % CHIPS) + c

    def rs_copy(way, step, sub):
        return remote(
            rs_send.at[way, step, sub], rs_recv.at[way, step, sub],
            rs_ssem.at[way, step, sub], rs_rsem.at[way, step, sub], right if way == 0 else left,
        )

    locals_[8].wait()
    attend((y + 4) % CHIPS, 0)
    locals_[9].wait()
    pairs[5].wait_recv()

    def first_body(j, carry):
        for way in range(2):
            sub = j + 2 * way
            rs_send[way, 0, sub] = project(sub).astype(bf16)
            rs_copy(way, 0, sub).start()
        return carry
    lax.fori_loop(0, 2, first_body, 0)

    def step_body(step, carry):
        away = 4 - step

        def attend_body(j, carry):
            attend((y + CHIPS + away * (1 - 2 * j)) % CHIPS, j)
            return carry
        lax.fori_loop(0, 2, attend_body, 0)

        def own_body(sub, carry):
            both = att[...].reshape(64, 512)
            own[sub] = jnp.dot(both, wbuf[:, lanes(sub, width)], preferred_element_type=f32)
            return carry
        lax.fori_loop(0, SUBS, own_body, 0)

        def sub_body(j, carry):
            for way in range(2):
                sub = (j + 2) % SUBS if way == 0 else j

                @pl.when((step > 1) | (j >= 2))
                def _():
                    rs_copy(way, step - 1, sub).wait_recv()

                added = own[sub, 32 * way : 32 * way + 32] + rs_recv[way, step - 1, sub].astype(f32)
                rs_send[way, step, sub] = added.astype(bf16)
                rs_copy(way, step, sub).start()
            return carry
        return lax.fori_loop(0, SUBS, sub_body, carry)

    lax.fori_loop(1, 4, step_body, 0)

    attend(y, 0)
    locals_[10].wait()

    def mine_body(sub, carry):
        hid[:, lanes(sub, width)] = project(sub) + resbuf[:, lanes(sub, width)].astype(f32)
        return carry
    lax.fori_loop(0, SUBS, mine_body, 0)

    def last_body(j, carry):
        for way in range(2):
            sub = (j + 2) % SUBS if way == 0 else j
            rs_copy(way, 3, sub).wait_recv()
            hid[:, lanes(sub, width)] += rs_recv[way, 3, sub].astype(f32)
        return carry
    lax.fori_loop(0, SUBS, last_body, 0)

    for copy in qd_copies + kv_copies + pairs:
        copy.wait_send()

    @pl.when(c != half)
    def _():
        qd_pair.wait_send()

    for j in range(4):
        @pl.when(jnp.logical_not((c == 1) & (y == 4 + j)))
        def _():
            dec_copies[j].wait_send()

    for j in range(2):
        for way in range(2):
            rs_copy(way, 0, j + 2 * way).wait_send()

    def rs_done(n, carry):
        for way in range(2):
            rs_copy(way, 1 + n // SUBS, n % SUBS).wait_send()
        return carry
    lax.fori_loop(0, 3 * SUBS, rs_done, 0)


def finish(hid, gain, out_res, out_norm):
    hidden = hid[...]
    out_res[...] = hidden.astype(bf16)
    mean_square = jnp.sum(hidden * hidden, axis=1, keepdims=True) * (1.0 / hidden.shape[1])
    out_norm[...] = (hidden * lax.rsqrt(mean_square + 1e-05) * gain[...]).astype(bf16)


def per_device(
    prompt_queries, prompt_entries, history_cache, decode_queries, decode_entries, decode_cache,
    decode_lengths, prompt_start, out_weight, residual, norm_gain,
):
    hbm = pl.BlockSpec(memory_space=pltpu.HBM)
    vmem = pl.BlockSpec(memory_space=pltpu.VMEM)
    span = history_cache.shape[1]
    entries = prompt_entries.shape[1]
    tokens, width = residual.shape
    dma = pltpu.SemaphoreType.DMA
    hidden = pl.pallas_call(
        kernel,
        out_shape=jax.ShapeDtypeStruct((tokens, width), f32),
        in_specs=[hbm] * 10,
        out_specs=vmem,
        scratch_shapes=[
            pltpu.SMEM(prompt_start.shape, jnp.int32),
            pltpu.SMEM(decode_lengths.shape, jnp.int32),
            pltpu.VMEM((2, span + 32, 512), bf16),
            pltpu.VMEM((entries, 2, 512), bf16),
            pltpu.VMEM((2, GROUP, span + 32, 128), bf16),
            pltpu.VMEM((4, 512, 128), bf16),
            pltpu.VMEM((2, 2, 16, 48, 256), bf16),
            pltpu.VMEM((8, 16, 256), bf16),
            pltpu.VMEM((512, width), bf16),
            pltpu.VMEM((tokens, width), bf16),
            pltpu.VMEM((2, 16, 128), bf16),
            pltpu.VMEM((4, 2, 64, 128), bf16),
            pltpu.VMEM((CHIPS, 2, 64, 128), bf16),
            pltpu.VMEM((2, 32, 512), bf16),
            pltpu.VMEM((SUBS, 64, width // SUBS), f32),
            pltpu.VMEM((2, 4, SUBS, 32, width // SUBS), bf16),
            pltpu.VMEM((2, 4, SUBS, 32, width // SUBS), bf16),
            dma((13,)), dma((8,)), dma((8,)), dma((16,)), dma((16,)), dma((6,)), dma((6,)),
            dma((4,)), dma((8,)), dma((2, 4, SUBS)), dma((2, 4, SUBS)),
        ],
        compiler_params=pltpu.CompilerParams(collective_id=0, has_side_effects=True),
    )(
        prompt_start, decode_lengths, prompt_queries, prompt_entries.transpose(1, 0, 2), history_cache,
        decode_queries, decode_entries, decode_cache, out_weight, residual,
    )
    shape = jax.ShapeDtypeStruct(residual.shape, residual.dtype)
    return pl.pallas_call(
        finish, out_shape=(shape, shape), in_specs=[vmem, vmem], out_specs=(vmem, vmem),
    )(hidden, norm_gain.reshape(1, -1))


def solution(mesh):
    placed = (
        P("rep", "tp"),
        P("rep", "tp", None),
        P("rep", "tp", None),
        P("rep", "tp"),
        P("rep", None, None),
        P("rep", None, "tp", None),
        P("rep"),
        P("rep"),
        P("tp", None),
        P("tp", "rep"),
        P(None),
    )
    return jax.shard_map(
        per_device, mesh=mesh, in_specs=placed, out_specs=(P("tp", "rep"), P("tp", "rep")),
        check_vma=False,
    )
```

time: 57.5 us -> 52.1 us (0.906)
  local copies, waits for them, and re-layouts: 4.81 us -> 0 us
    unnamed x3 -> x0, local copies, waits for them, and re-layouts: 4.81 us -> none
    pallas_call x1 -> x2, Pallas kernels: 51.2 us -> 50.7 us  [the longest x1 48.8 us: per_device(): pl.pallas_call(kernel, out_shape=jax.ShapeDtypeStruct((tokens, width), f3...]
where the time goes in v2:
time: 52.1 us; the launch traced here: 52 us
  Pallas kernels  50.7 us (97%)
  between operations  1.29 us (2%)
    pallas_call x1, Pallas kernels, per_device(): pl.pallas_call(kernel, out_shape=jax.ShapeDtypeStruct((tokens, width), f3...  48.8 us
    pallas_call x1, Pallas kernels, per_device(): pl.pallas_call(finish, out_shape=(shape, shape), in_specs=[vmem, vmem], o...  1.94 us

profile of v2, /device:TPU:1, one launch (start us, length us, event | category | flops | bytes accessed | tf_op | source)
XLA Modules:
  0.0 52.0 jit_solution(6171389981754312279)
XLA Ops:
  1.3 48.8 %shard_map.122.hid = f32[32,4096]{1,0:T(8,128)} custom-call(s32[1]{0:T(128)S(6)} %copy.13.start_in, s32[16]{0:T(128)} %lengths_in.1, bf16[496,256]{1,0:T(8,128)(2,1)} %pq.1, bf16[31,2,512]{2,1,0:T(2,128)(2,1)} %bitcast.2, bf16[2,64,512]{2,1,0:T(8,128)(2,1)} %hist.1, bf16[16,256]{1,0:T(8,128)(2,1)} %dq.1, bf16[2,16,512]{2,1,0:T(8,128)(2,1)} %de.1, ...), custom_call_target="tpu_custom_call" | custom-call | tf_op jit(solution)/shard_map/pallas_call | solution.py:390
  50.1 1.9 %shard_map.123 = (bf16[32,4096]{1,0:T(8,128)(2,1)}, bf16[32,4096]{1,0:T(8,128)(2,1)}) custom-call(f32[32,4096]{1,0:T(8,128)} %shard_map.122.hid, f32[1,4096]{1,0:T(1,128)} %bitcast.3), custom_call_target="tpu_custom_call" | custom-call | tf_op jit(solution)/shard_map/pallas_call | solution.py:422

commit v3 on v2

--- a/solution.py
+++ b/solution.py
@@ -8,7 +8,8 @@
 HEAD_DIM = 128
 CHIPS = 8
 GROUP = 16
-SUBS = 4
+SUBS = 2
+HALF = SUBS // 2
 MESH = pl.DeviceIdType.MESH
 LOWEST = -(2.0**100)
 FACTOR = HEAD_DIM**-0.5 * 1.4426950408889634
@@ -32,7 +33,7 @@
     start_ref, lengths_ref, stage, pbuf, kv, qbuf, dbuf, qd, wbuf, resbuf, fresh,
     dec_send, dec_recv, att, own, rs_send, rs_recv,
     local_sem, qd_ssem, qd_rsem, kv_ssem, kv_rsem, pair_ssem, pair_rsem,
-    dec_ssem, dec_rsem, rs_ssem, rs_rsem,
+    dec_ssem, dec_rsem, rs_ssem, rs_rsem, plane_sem,
 ):
     t = lax.axis_index("tp")
     y = t // 2
@@ -62,9 +63,9 @@
         return pl.ds(pl.multiple_of(index * size, size), size)
 
     locals_ = [
-        local(hist, stage.at[:, pl.ds(0, span), :], 0),
+        local(start_in, start_ref, 0),
         local(pe, pbuf, 1),
-        local(hist.at[:, :, lanes(head, 128)], kv.at[:, t, pl.ds(0, span), :], 2),
+        local(hist.at[:, :, lanes(head, 128)], kv.at[t, :, pl.ds(0, span), :], 2),
         local(dc.at[:, :, :, lanes(c, 256)], dbuf.at[c], 3),
     ]
     for i in range(2):
@@ -73,31 +74,80 @@
         locals_.append(local(dq.at[:, columns], qbuf.at[2 * c + i, pl.ds(rows, 16), :], 6 + i))
     locals_ += [
         local(de.at[:, :, lanes(head, 128)], fresh, 8),
-        local(w, wbuf.at[pl.ds(pl.multiple_of(256 * c, 256), 256), :], 9),
+        local(w.at[:, pl.ds(0, width)], wbuf.at[0, pl.ds(pl.multiple_of(256 * c, 256), 256), :], 9),
         local(res, resbuf, 10),
-        local(start_in, start_ref, 11),
-        local(lengths_in, lengths_ref, 12),
+        local(lengths_in, lengths_ref, 11),
     ]
-    for copy in locals_:
+    own_weights = [locals_[9]] + [
+        local(w.at[:, pl.ds(sub * width, width)], wbuf.at[sub, pl.ds(pl.multiple_of(256 * c, 256), 256), :], 15 + sub)
+        for sub in range(1, SUBS)
+    ]
+    staged = [
+        local(hist.at[:, :, pl.ds(128 * h, 128)], stage.at[h, :, pl.ds(0, span), :], 12 + h)
+        for h in range(4)
+    ]
+    for copy in [locals_[1]] + staged + locals_[:1] + locals_[2:] + own_weights[1:]:
         copy.start()
 
     barrier = pltpu.get_barrier_semaphore()
-    for k in range(1, GROUP):
+    for k in range(1, CHIPS):
         pl.semaphore_signal(
-            barrier, inc=1, device_id={"tp": (t + k) % GROUP}, device_id_type=MESH
-        )
-
-    locals_[0].wait()
+            barrier, inc=1, device_id={"tp": 2 * ((y + k) % CHIPS) + c}, device_id_type=MESH
+        )
+    pl.semaphore_signal(barrier, inc=1, device_id={"tp": partner}, device_id_type=MESH)
+
     locals_[1].wait()
     for i in range(2):
-        stage[i, span : span + 32, :] = jnp.concatenate(
+        block = jnp.concatenate(
             [pbuf[:, i, :], jnp.zeros((32 - entries, pbuf.shape[2]), bf16)], axis=0
         )
+        for h in range(4):
+            stage[h, i, span : span + 32, :] = block[:, 128 * h : 128 * h + 128]
     for i in range(2):
-        kv[i, t, span : span + 32, :] = stage[i, span : span + 32, lanes(head, 128)]
-    rs_recv[0, 0, 2:4] = jnp.zeros((2, 32, width), bf16)
-    rs_recv[1, 0, 0:2] = jnp.zeros((2, 32, width), bf16)
-    pl.semaphore_wait(barrier, GROUP - 1)
+        kv[t, i, span : span + 32, :] = stage[head, i, span : span + 32, :]
+    for copy in staged:
+        copy.wait()
+    rs_recv[0, 0, HALF:] = jnp.zeros((HALF, 32, width), bf16)
+    rs_recv[1, 0, :HALF] = jnp.zeros((HALF, 32, width), bf16)
+    pl.semaphore_wait(barrier, CHIPS)
+    pl.semaphore_signal(plane_sem, inc=1, device_id={"tp": partner}, device_id_type=MESH)
+
+    kv_copies = []
+
+    def send_kv(src, slot, device):
+        n = len(kv_copies)
+        copy = remote(src, kv.at[slot], kv_ssem.at[n], kv_rsem.at[slot], device)
+        copy.start()
+        kv_copies.append(copy)
+
+    def own_block(there):
+        return stage.at[there // 2]
+
+    mate = chip(-1)
+    for steps in (3, -3, 2, -2, 1, -1):
+        there = chip(steps)
+        send_kv(own_block(there), t, 2 * there + c)
+
+    pairs = [remote(dc.at[:, :, :, lanes(1 - c, 256)], dbuf.at[c], pair_ssem.at[0], pair_rsem.at[0], partner)]
+    for i in range(2):
+        columns = pl.ds(128 * i, 128)
+        pairs.append(
+            remote(pq.at[:, columns], qbuf.at[2 * c + i, pl.ds(0, rows), :],
+                   pair_ssem.at[1 + i], pair_rsem.at[1 + i], partner)
+        )
+        pairs.append(
+            remote(dq.at[:, columns], qbuf.at[2 * c + i, pl.ds(rows, 16), :],
+                   pair_ssem.at[3 + i], pair_rsem.at[3 + i], partner)
+        )
+    for sub in range(SUBS):
+        pairs.append(
+            remote(w.at[:, pl.ds(sub * width, width)], wbuf.at[sub, pl.ds(pl.multiple_of(256 * c, 256), 256), :],
+                   pair_ssem.at[5 + sub], pair_rsem.at[5 + sub], partner)
+        )
+    weights_in = pairs[5:]
+    for copy in pairs[:5]:
+        copy.start()
+    pl.semaphore_wait(plane_sem, 1)
 
     place = t - 8 * half
     qd_copies = []
@@ -116,52 +166,29 @@
     def _():
         qd_pair.start()
 
-    kv_copies = []
-
-    def send_kv(src, slot, device):
-        n = len(kv_copies)
-        copy = remote(src, kv.at[:, slot], kv_ssem.at[n], kv_rsem.at[slot], device)
-        copy.start()
-        kv_copies.append(copy)
-
-    def own_block(there):
-        return stage.at[:, :, lanes(there // 2, 128)]
-
-    mate = chip(-1)
-    for steps in (3, -2, 1, -1):
-        there = chip(steps)
-        send_kv(own_block(there), t, 2 * there + c)
-
-    pairs = [remote(dc.at[:, :, :, lanes(1 - c, 256)], dbuf.at[c], pair_ssem.at[0], pair_rsem.at[0], partner)]
-    for i in range(2):
-        columns = pl.ds(128 * i, 128)
-        pairs.append(
-            remote(pq.at[:, columns], qbuf.at[2 * c + i, pl.ds(0, rows), :],
-                   pair_ssem.at[1 + i], pair_rsem.at[1 + i], partner)
-        )
-        pairs.append(
-            remote(dq.at[:, columns], qbuf.at[2 * c + i, pl.ds(rows, 16), :],
-                   pair_ssem.at[3 + i], pair_rsem.at[3 + i], partner)
-        )
-    pairs.append(
-        remote(w, wbuf.at[pl.ds(pl.multiple_of(256 * c, 256), 256), :],
-               pair_ssem.at[5], pair_rsem.at[5], partner)
-    )
-    for copy in pairs:
-        copy.start()
     send_kv(own_block(y), t, partner)
+    order = [n + HALF * way for n in range(HALF) for way in range(2)]
+    for n in order[:HALF]:
+        weights_in[n].start()
 
     def wait_kv(slot):
-        pltpu.make_async_copy(kv.at[:, slot], kv.at[:, slot], kv_rsem.at[slot]).wait()
-
-    for steps in (2, 1, 3):
+        pltpu.make_async_copy(kv.at[slot], kv.at[slot], kv_rsem.at[slot]).wait()
+
+    def take_kv(steps):
         slot = 2 * chip(steps) + c
         wait_kv(slot)
-        send_kv(kv.at[:, slot], slot, 2 * mate + c)
-        send_kv(kv.at[:, slot], slot, partner)
+        if steps == 3:
+            send_kv(kv.at[slot], slot, 2 * mate + c)
+        send_kv(kv.at[slot], slot, partner)
+
+    take_kv(3)
+    take_kv(-3)
+    for n in order[HALF:]:
+        weights_in[n].start()
+    take_kv(2)
+    take_kv(-2)
 
     locals_[11].wait()
-    locals_[12].wait()
     row_b = iota((128, 1), 0) & 15
     limit = jnp.zeros((128, 1), jnp.int32)
     for b in range(16):
@@ -214,13 +241,12 @@
         def _():
             copy.start()
 
-    for steps in (-1, -3, -2, -4):
-        slot = 2 * chip(steps) + c
-        wait_kv(slot)
-        send_kv(kv.at[:, slot], slot, partner)
+    for steps in (1, -1, -4):
+        take_kv(steps)
     col = iota((1, 1536), 1)
     owner = (col * 683) >> 16
     place = col - 96 * owner
+    locals_[0].wait()
     start = start_ref[0]
     from_history = jnp.where(owner * span + place < start, -1, NEVER)
     from_prompt = jnp.where(place < span + entries, owner * entries + place - span, NEVER)
@@ -262,8 +288,8 @@
     def attend(d, slot):
         row = pl.multiple_of(64 * d + 32 * c, 32)
         q = qbuf[:, pl.ds(row, 32), :].reshape(128, 128)
-        keys = kv[0].reshape(1536, 128)
-        values = kv[1].reshape(1536, 128)
+        keys = kv[:, 0].reshape(1536, 128)
+        values = kv[:, 1].reshape(1536, 128)
         scores = jnp.where(first_row <= row + row32, dot_t(q, keys), LOWEST)
         top = jnp.max(scores, axis=1, keepdims=True)
         weights = jnp.exp2((scores - top) * FACTOR)
@@ -278,7 +304,7 @@
             decode_rows(slot)
 
     def project(sub):
-        return jnp.dot(att[0], wbuf[:, lanes(sub, width)], preferred_element_type=f32)
+        return jnp.dot(att[0], wbuf[sub], preferred_element_type=f32)
 
     right, left = 2 * ((y + 1) % CHIPS) + c, 2 * ((y + 7) % CHIPS) + c
 
@@ -290,16 +316,18 @@
 
     locals_[8].wait()
     attend((y + 4) % CHIPS, 0)
-    locals_[9].wait()
-    pairs[5].wait_recv()
+    for copy in own_weights:
+        copy.wait()
+    for copy in weights_in:
+        copy.wait_recv()
 
     def first_body(j, carry):
         for way in range(2):
-            sub = j + 2 * way
+            sub = j + HALF * way
             rs_send[way, 0, sub] = project(sub).astype(bf16)
             rs_copy(way, 0, sub).start()
         return carry
-    lax.fori_loop(0, 2, first_body, 0)
+    lax.fori_loop(0, HALF, first_body, 0)
 
     def step_body(step, carry):
         away = 4 - step
@@ -311,15 +339,15 @@
 
         def own_body(sub, carry):
             both = att[...].reshape(64, 512)
-            own[sub] = jnp.dot(both, wbuf[:, lanes(sub, width)], preferred_element_type=f32)
+            own[sub] = jnp.dot(both, wbuf[sub], preferred_element_type=f32)
             return carry
         lax.fori_loop(0, SUBS, own_body, 0)
 
         def sub_body(j, carry):
             for way in range(2):
-                sub = (j + 2) % SUBS if way == 0 else j
-
-                @pl.when((step > 1) | (j >= 2))
+                sub = (j + HALF) % SUBS if way == 0 else j
+
+                @pl.when((step > 1) | (j >= HALF))
                 def _():
                     rs_copy(way, step - 1, sub).wait_recv()
 
@@ -341,7 +369,7 @@
 
     def last_body(j, carry):
         for way in range(2):
-            sub = (j + 2) % SUBS if way == 0 else j
+            sub = (j + HALF) % SUBS if way == 0 else j
             rs_copy(way, 3, sub).wait_recv()
             hid[:, lanes(sub, width)] += rs_recv[way, 3, sub].astype(f32)
         return carry
@@ -359,9 +387,9 @@
         def _():
             dec_copies[j].wait_send()
 
-    for j in range(2):
+    for j in range(HALF):
         for way in range(2):
-            rs_copy(way, 0, j + 2 * way).wait_send()
+            rs_copy(way, 0, j + HALF * way).wait_send()
 
     def rs_done(n, carry):
         for way in range(2):
@@ -395,13 +423,13 @@
         scratch_shapes=[
             pltpu.SMEM(prompt_start.shape, jnp.int32),
             pltpu.SMEM(decode_lengths.shape, jnp.int32),
-            pltpu.VMEM((2, span + 32, 512), bf16),
+            pltpu.VMEM((4, 2, span + 32, 128), bf16),
             pltpu.VMEM((entries, 2, 512), bf16),
-            pltpu.VMEM((2, GROUP, span + 32, 128), bf16),
+            pltpu.VMEM((GROUP, 2, span + 32, 128), bf16),
             pltpu.VMEM((4, 512, 128), bf16),
             pltpu.VMEM((2, 2, 16, 48, 256), bf16),
             pltpu.VMEM((8, 16, 256), bf16),
-            pltpu.VMEM((512, width), bf16),
+            pltpu.VMEM((SUBS, 512, width // SUBS), bf16),
             pltpu.VMEM((tokens, width), bf16),
             pltpu.VMEM((2, 16, 128), bf16),
             pltpu.VMEM((4, 2, 64, 128), bf16),
@@ -410,8 +438,8 @@
             pltpu.VMEM((SUBS, 64, width // SUBS), f32),
             pltpu.VMEM((2, 4, SUBS, 32, width // SUBS), bf16),
             pltpu.VMEM((2, 4, SUBS, 32, width // SUBS), bf16),
-            dma((13,)), dma((8,)), dma((8,)), dma((16,)), dma((16,)), dma((6,)), dma((6,)),
-            dma((4,)), dma((8,)), dma((2, 4, SUBS)), dma((2, 4, SUBS)),
+            dma((15 + SUBS,)), dma((8,)), dma((8,)), dma((16,)), dma((16,)), dma((5 + SUBS,)), dma((5 + SUBS,)),
+            dma((4,)), dma((8,)), dma((2, 4, SUBS)), dma((2, 4, SUBS)), pltpu.SemaphoreType.REGULAR,
         ],
         compiler_params=pltpu.CompilerParams(collective_id=0, has_side_effects=True),
     )(

time: 52.1 us -> 50.8 us (0.975)
  Pallas kernels: 50.7 us -> 49.4 us
    pallas_call x1, Pallas kernels: 48.8 us -> 47.4 us  [per_device(): pl.pallas_call(kernel, out_shape=jax.ShapeDtypeStruct((tokens, width), f3...]
where the time goes in v3:
time: 50.8 us; the launch traced here: 50.7 us
  Pallas kernels  49.4 us (97%)
  between operations  1.29 us (3%)
    pallas_call x1, Pallas kernels, per_device(): pl.pallas_call(kernel, out_shape=jax.ShapeDtypeStruct((tokens, width), f3...  47.4 us
    pallas_call x1, Pallas kernels, per_device(): pl.pallas_call(finish, out_shape=(shape, shape), in_specs=[vmem, vmem], o...  1.94 us

profile of v3, /device:TPU:1, one launch (start us, length us, event | category | flops | bytes accessed | tf_op | source)
XLA Modules:
  0.0 50.7 jit_solution(5077746129507179802)
XLA Ops:
  1.3 47.4 %shard_map.122.hid = f32[32,4096]{1,0:T(8,128)} custom-call(s32[1]{0:T(128)S(6)} %copy.13.start_in, s32[16]{0:T(128)} %lengths_in.1, bf16[496,256]{1,0:T(8,128)(2,1)} %pq.1, bf16[31,2,512]{2,1,0:T(2,128)(2,1)} %bitcast.2, bf16[2,64,512]{2,1,0:T(8,128)(2,1)} %hist.1, bf16[16,256]{1,0:T(8,128)(2,1)} %dq.1, bf16[2,16,512]{2,1,0:T(8,128)(2,1)} %de.1, ...), custom_call_target="tpu_custom_call" | custom-call | tf_op jit(solution)/shard_map/pallas_call | solution.py:418
  48.7 1.9 %shard_map.123 = (bf16[32,4096]{1,0:T(8,128)(2,1)}, bf16[32,4096]{1,0:T(8,128)(2,1)}) custom-call(f32[32,4096]{1,0:T(8,128)} %shard_map.122.hid, f32[1,4096]{1,0:T(1,128)} %bitcast.3), custom_call_target="tpu_custom_call" | custom-call | tf_op jit(solution)/shard_map/pallas_call | solution.py:450

commit v4 on v3

--- a/solution.py
+++ b/solution.py
@@ -112,6 +112,31 @@
     pl.semaphore_wait(barrier, CHIPS)
     pl.semaphore_signal(plane_sem, inc=1, device_id={"tp": partner}, device_id_type=MESH)
 
+    place = t - 8 * half
+    qd_copies = []
+    for k in range(1, CHIPS):
+        copy = remote(dq, qd.at[place], qd_ssem.at[k], qd_rsem.at[place], 2 * ((y + k) % CHIPS) + half)
+        qd_copies.append(copy)
+
+    def send_queries():
+        for copy in qd_copies:
+            copy.start()
+
+    qd_pair = remote(dq, qd.at[place], qd_ssem.at[0], qd_rsem.at[place], partner)
+    qd_own = pltpu.make_async_copy(dq, qd.at[place], qd_rsem.at[place])
+
+    @pl.when(c == half)
+    def _():
+        qd_own.start()
+
+    @pl.when(c != half)
+    def _():
+        qd_pair.start()
+
+    @pl.when(c == half)
+    def _():
+        send_queries()
+
     kv_copies = []
 
     def send_kv(src, slot, device):
@@ -149,22 +174,9 @@
         copy.start()
     pl.semaphore_wait(plane_sem, 1)
 
-    place = t - 8 * half
-    qd_copies = []
-    for k in range(1, CHIPS):
-        copy = remote(dq, qd.at[place], qd_ssem.at[k], qd_rsem.at[place], 2 * ((y + k) % CHIPS) + half)
-        copy.start()
-        qd_copies.append(copy)
-    qd_pair = remote(dq, qd.at[place], qd_ssem.at[0], qd_rsem.at[place], partner)
-    qd_own = pltpu.make_async_copy(dq, qd.at[place], qd_rsem.at[place])
-
-    @pl.when(c == half)
-    def _():
-        qd_own.start()
-
     @pl.when(c != half)
     def _():
-        qd_pair.start()
+        send_queries()
 
     send_kv(own_block(y), t, partner)
     order = [n + HALF * way for n in range(HALF) for way in range(2)]

time: 50.8 us -> 49.7 us (0.978)
  Pallas kernels: 49.4 us -> 48.2 us
    pallas_call x1, Pallas kernels: 47.4 us -> 46.3 us  [per_device(): pl.pallas_call(kernel, out_shape=jax.ShapeDtypeStruct((tokens, width), f3...]
where the time goes in v4:
time: 49.7 us; the launch traced here: 49.5 us
  Pallas kernels  48.2 us (97%)
  between operations  1.29 us (3%)
    pallas_call x1, Pallas kernels, per_device(): pl.pallas_call(kernel, out_shape=jax.ShapeDtypeStruct((tokens, width), f3...  46.3 us
    pallas_call x1, Pallas kernels, per_device(): pl.pallas_call(finish, out_shape=(shape, shape), in_specs=[vmem, vmem], o...  1.94 us

profile of v4, /device:TPU:1, one launch (start us, length us, event | category | flops | bytes accessed | tf_op | source)
XLA Modules:
  0.0 49.5 jit_solution(6547826077238409983)
XLA Ops:
  1.3 46.3 %shard_map.122.hid = f32[32,4096]{1,0:T(8,128)} custom-call(s32[1]{0:T(128)S(6)} %copy.13.start_in, s32[16]{0:T(128)} %lengths_in.1, bf16[496,256]{1,0:T(8,128)(2,1)} %pq.1, bf16[31,2,512]{2,1,0:T(2,128)(2,1)} %bitcast.2, bf16[2,64,512]{2,1,0:T(8,128)(2,1)} %hist.1, bf16[16,256]{1,0:T(8,128)(2,1)} %dq.1, bf16[2,16,512]{2,1,0:T(8,128)(2,1)} %de.1, ...), custom_call_target="tpu_custom_call" | custom-call | tf_op jit(solution)/shard_map/pallas_call | solution.py:430
  47.6 1.9 %shard_map.123 = (bf16[32,4096]{1,0:T(8,128)(2,1)}, bf16[32,4096]{1,0:T(8,128)(2,1)}) custom-call(f32[32,4096]{1,0:T(8,128)} %shard_map.122.hid, f32[1,4096]{1,0:T(1,128)} %bitcast.3), custom_call_target="tpu_custom_call" | custom-call | tf_op jit(solution)/shard_map/pallas_call | solution.py:462
